TPU v7x, 128 devices: a whole 4x4x4 slice. The times are simulated.
128 devices in a mesh: aux: 8 (over z_hi, y), pair: 16 (over z_lo, x, core).
Axes of the slice: x: 4, y: 4, z: 4 (z_hi: 2, z_lo: 2; z = z_hi * 2 + z_lo), core: 2. Of those that a mesh axis runs over, the one named last changes fastest.
Arguments:
- m_panels: bfloat16 [40000, 16384], P('aux', 'pair'), may hold values from -6 to 6
- lower_cols: bfloat16 [2, 512, 40000], P(None, 'pair', 'aux'), may hold values from -0.2 to 0.2, as said below
- diag_inverses: float32 [2, 512, 512], replicated, may hold values from -0.2 to 2, as said below
Outputs:
- remainder: bfloat16 [40000, 16384], P('aux', 'pair')
- solved: bfloat16 [2, 512, 16384], P(None, None, 'pair')
Inputs may be any that keep to these rules, and one draw needn't show every extreme that they name: lower_cols[k] is zero in the pivot rows of panels 0 to k (the factor is lower triangular and its diagonal blocks are given by their inverses). Each diag_inverses[k] is lower triangular.
All inputs are finite; a program needn't handle non-finite values.
Results may differ from a plain program's by a relative error of at most 0.0047.
Values may be sent and summed in bfloat16 or wider, within the bound.
A program may use at most 192 MiB of HBM per device.

v0:
```python
import functools

import jax
import jax.numpy as jnp
from jax import lax
from jax.experimental import pallas as pl
from jax.experimental.pallas import tpu as pltpu
from jax.sharding import PartitionSpec as P

MESH = pl.DeviceIdType.MESH
TYPES = "AABAABAA"
NP = 8
ORDER = (
    (0, (('Py+', 0, 1), ('Py+', 0, 0), ('Py-', 0, 0), ('Py-', 0, 3), ('X', 0, 5), ('X', 0, 6), ('X', 0, 7))),
    (1, (('Py+', 1, 0), ('Py+', 1, 2), ('Py-', 1, 0), ('Py-', 1, 1), ('X', 1, 4), ('X', 1, 6), ('X', 1, 7))),
    ('od', 0),
    ('od', 1),
    ('od', 2),
    ('od', 3),
    ('od', 4),
    ('od', 5),
    ('od', 6),
    ('od', 7),
    ('ou', 0),
    ('ou', 1),
    ('oz', 0),
    ('ou', 2),
    ('oz', 1),
    (0, (('Py+', 0, 2), ('Py-', 0, 4), ('R', 0, 5))),
    (1, (('Py+', 1, 3), ('Py-', 1, 3), ('R', 1, 4))),
    (4, (('R', 0, 5),)),
    (5, (('R', 1, 4),)),
    ('oz', 2),
    ('g', 0),
    ('f', 0),
    ('oz', 'V'),
    (0, (('P', 1, 0), ('R', 0, 6), ('Py+', 0, 3))),
    (1, (('R', 1, 6), ('P', 0, 0), ('Py-', 1, 4))),
    (2, (('P', 1, 0),)),
    (3, (('P', 0, 0),)),
    (4, (('R', 0, 6),)),
    (5, (('R', 1, 6),)),
    ('f', 1),
    ('g', 1),
    (0, (('R', 0, 7), ('P', 1, 1), ('Py+', 0, 4), ('Py-', 0, 5))),
    (1, (('R', 1, 7), ('P', 0, 1), ('Py-', 1, 5))),
    (2, (('P', 1, 2),)),
    (3, (('P', 0, 3),)),
    (4, (('R', 0, 7),)),
    (5, (('R', 1, 7),)),
    ('z', 0),
    ('g', 2),
    ('f', 2),
    (4, (('P', 0, 5),)),
    (5, (('P', 1, 4),)),
    (6, (('R', 1, 0),)),
    (7, (('R', 0, 0),)),
    ('z', 1),
    (0, (('P', 1, 3), ('Py+', 0, 5))),
    (1, (('P', 0, 2), ('Py+', 1, 5), ('Py-', 1, 7))),
    (2, (('R', 1, 0), ('P', 0, 0), ('P', 1, 3))),
    (3, (('R', 0, 0), ('P', 0, 4))),
    ('ou', 3),
    ('oz', 3),
    (1, (('P', 0, 3),)),
    (2, (('R', 1, 2),)),
    (3, (('R', 0, 3), ('P', 1, 2))),
    (4, (('P', 0, 6), ('R', 1, 1))),
    (5, (('P', 1, 6), ('R', 0, 1))),
    (6, (('R', 1, 2),)),
    (7, (('R', 0, 3),)),
    ('z', 2),
    ('z', 'V'),
    (0, (('P', 1, 4), ('Py+', 0, 6), ('R', 1, 1))),
    (1, (('Py+', 1, 6), ('R', 0, 1))),
    (2, (('P', 0, 3), ('P', 0, 1))),
    (3, (('P', 1, 1),)),
    (4, (('P', 0, 7),)),
    (5, (('P', 1, 7), ('R', 0, 2))),
    (6, (('P', 1, 4),)),
    ('ou', 4),
    (3, (('P', 1, 3),)),
    (4, (('P', 1, 4),)),
    (5, (('P', 0, 5),)),
    (6, (('R', 1, 3),)),
    (7, (('P', 0, 5), ('R', 0, 4))),
    ('g', 3),
    ('oz', 4),
    (0, (('P', 1, 5), ('Py+', 0, 7), ('Py-', 0, 6))),
    (1, (('Py+', 1, 7),)),
    (2, (('P', 0, 4), ('P', 0, 2))),
    (3, (('P', 1, 0), ('P', 0, 5))),
    (5, (('P', 0, 6),)),
    ('g', 'V'),
    (1, (('P', 0, 4),)),
    ('zg', 2),
    (6, (('P', 1, 0), ('P', 1, 6))),
    (7, (('P', 0, 0),)),
    ('o', 0),
    (2, (('R', 1, 3),)),
    (3, (('R', 0, 4),)),
    (7, (('P', 0, 6),)),
    ('zf', 0),
    ('f', 'V'),
    ('ou', 5),
    (0, (('P', 1, 2),)),
    ('oz', 5),
    (0, (('P', 1, 7), ('Py-', 0, 7))),
    (1, (('P', 0, 5),)),
    (2, (('P', 1, 1), ('P', 1, 5))),
    (3, (('P', 0, 1), ('P', 1, 4))),
    (4, (('P', 1, 7),)),
    ('zf', 1),
    ('zf', 2),
    (7, (('P', 0, 3),)),
    ('g', 4),
    ('f', 3),
    (1, (('R', 0, 2),)),
    (5, (('P', 0, 7),)),
    (6, (('P', 1, 2), ('P', 0, 5))),
    (7, (('P', 1, 4), ('P', 0, 7))),
    ('zf', 'V'),
    (2, (('P', 0, 5),)),
    (3, (('P', 0, 2),)),
    (4, (('P', 1, 1),)),
    (5, (('P', 0, 1),)),
    ('zg', 0),
    (1, (('P', 0, 6),)),
    (2, (('P', 1, 6),)),
    (3, (('P', 1, 5),)),
    (4, (('P', 0, 0),)),
    (5, (('P', 1, 0),)),
    (6, (('P', 0, 0),)),
    (7, (('P', 0, 4),)),
    ('z', 3),
    ('f', 4),
    ('zo', 0),
    (7, (('P', 1, 0),)),
    ('o', 1),
    (6, (('P', 1, 3), ('R', 1, 5))),
    ('ou', 6),
    (6, (('P', 0, 6),)),
    ('done', 0),
    (7, (('P', 1, 7),)),
    ('z', 4),
    ('o', 2),
    (1, (('P', 0, 7),)),
    (2, (('P', 1, 4),)),
    (3, (('P', 0, 6),)),
    ('f', 5),
    (2, (('R', 1, 5),)),
    (4, (('P', 0, 3),)),
    (5, (('P', 0, 2), ('P', 1, 2))),
    (6, (('P', 0, 3),)),
    ('g', 5),
    (7, (('P', 1, 6),)),
    ('zg', 1),
    (4, (('P', 0, 1),)),
    ('zo', 1),
    (5, (('P', 1, 1),)),
    (6, (('P', 0, 7),)),
    (7, (('P', 1, 1),)),
    ('done', 1),
    ('o', 'V'),
    ('zg', 'V'),
    ('oz', 6),
    (2, (('P', 1, 7),)),
    ('zo', 'V'),
    (3, (('P', 1, 6), ('P', 0, 7))),
    ('ou', 7),
    (4, (('P', 0, 4),)),
    ('oz', 7),
    (5, (('P', 1, 3),)),
    (6, (('P', 0, 4),)),
    ('z', 5),
    (7, (('P', 1, 2),)),
    ('zf', 3),
    (5, (('P', 0, 0),)),
    (6, (('P', 0, 1),)),
    ('o', 3),
    ('zo', 2),
    (2, (('P', 0, 7), ('P', 0, 6))),
    (3, (('P', 1, 7),)),
    (4, (('P', 0, 2),)),
    (6, (('P', 1, 5),)),
    ('zf', 4),
    (0, (('P', 1, 6),)),
    (4, (('P', 1, 0),)),
    ('zg', 3),
    ('done', 2),
    (5, (('P', 0, 3),)),
    (6, (('P', 1, 7), ('P', 0, 2))),
    (7, (('P', 1, 3), ('P', 0, 1))),
    ('g', 6),
    ('o', 4),
    ('done', 'V'),
    ('f', 6),
    ('o', 5),
    (4, (('P', 1, 6), ('P', 1, 3))),
    (6, (('P', 1, 1),)),
    ('f', 7),
    ('zg', 4),
    ('zg', 5),
    ('g', 7),
    ('zf', 5),
    ('z', 6),
    (5, (('P', 0, 4),)),
    (7, (('P', 0, 2),)),
    ('S', 0),
    (7, (('P', 1, 5),)),
    ('z', 7),
    (4, (('P', 1, 2),)),
    ('zo', 3),
    (5, (('P', 1, 5),)),
    ('A', 0),
    ('o', 6),
    ('A', 1),
    ('zo', 4),
    ('done', 3),
    ('o', 7),
    ('zf', 6),
    ('A', 2),
    ('zo', 5),
    ('zg', 6),
    ('A', 3),
    ('zg', 7),
    ('done', 4),
    ('zf', 7),
    ('A', 4),
    ('zo', 6),
    (4, (('P', 1, 5),)),
    ('S', 1),
    ('zo', 7),
    ('done', 6),
    ('done', 5),
    ('B', 0),
    ('done', 7),
    ('B', 1),
    ('B', 2),
    ('B', 3),
    ('B', 4),
)
ROUTE = {
    (0, 0): (3, {0: {0: ['y+', 'y-'], 3: ['y-']}, 1: {3: ['y+', 'y-'], 0: ['y+']}}),
    (0, 1): (1, {0: {0: ['y+'], 1: ['y+'], 2: ['y+']}, 1: {1: ['y+', 'y-'], 0: ['y-']}}),
    (0, 2): (1, {0: {0: ['y+'], 1: ['y+'], 2: ['y+']}, 1: {1: ['y+', 'y-'], 0: ['y-']}}),
    (0, 3): (3, {0: {0: ['y+', 'y-'], 3: ['y-']}, 1: {3: ['y+', 'y-'], 0: ['y+']}}),
    (0, 4): (3, {0: {0: ['y+', 'y-'], 3: ['y-']}, 1: {3: ['y+', 'y-'], 2: ['y-']}}),
    (0, 5): (0, {0: {0: ['y+', 'y-'], 3: ['y-']}, 1: {0: ['y+', 'y-'], 1: ['y+']}}),
    (0, 6): (0, {0: {0: ['y+', 'y-'], 3: ['y-']}, 1: {0: ['y+', 'y-'], 1: ['y+']}}),
    (0, 7): (0, {0: {0: ['y+', 'y-'], 1: ['y+']}, 1: {0: ['y+', 'y-'], 1: ['y+']}}),
    (1, 0): (2, {0: {1: ['y+', 'y-'], 2: ['y+']}, 1: {2: ['y+', 'y-'], 3: ['y+']}}),
    (1, 1): (0, {0: {1: ['y-'], 0: ['y-'], 3: ['y-']}, 1: {0: ['y+', 'y-'], 3: ['y-']}}),
    (1, 2): (2, {0: {1: ['y+'], 2: ['y+'], 3: ['y+']}, 1: {2: ['y+', 'y-'], 3: ['y+']}}),
    (1, 3): (2, {0: {1: ['y+', 'y-'], 2: ['y+']}, 1: {2: ['y+', 'y-'], 1: ['y-']}}),
    (1, 4): (1, {0: {1: ['y-'], 0: ['y-'], 3: ['y-']}, 1: {1: ['y+', 'y-'], 2: ['y+']}}),
    (1, 5): (2, {0: {1: ['y+', 'y-'], 0: ['y-']}, 1: {2: ['y+', 'y-'], 1: ['y-']}}),
    (1, 6): (1, {0: {1: ['y+'], 2: ['y+'], 3: ['y+']}, 1: {1: ['y+'], 2: ['y+'], 3: ['y+']}}),
    (1, 7): (1, {0: {1: ['y+', 'y-'], 2: ['y+']}, 1: {1: ['y-'], 0: ['y-'], 3: ['y-']}}),
}
CHUNKS = ((0, 640), (640, 640), (1280, 896), (2176, 640), (2816, 640), (3456, 896), (4352, 384), (4736, 264))
TAIL = (5, 6, 7)
Z, M, PL, O, ZM, ZP, ZO = range(7)


def kernel(m_hbm, l_hbm, d_hbm, out, solved, lbuf, pbuf, rbuf, vbuf, dbuf, acc,
           load_sem, l_recv, l_sib, l_send, v_recv, v_send, p_recv, r_recv, p_send):
    aux, pair = lax.axis_index("aux"), lax.axis_index("pair")
    zh, y = aux // 4, aux % 4
    zl, x, c = pair // 8, (pair // 2) % 4, pair % 2
    nb = l_hbm.shape[1]
    nrows = l_hbm.shape[2]
    nk = nb * 16
    nchunk = len(TYPES)
    piece = nk // NP
    half = piece // 2
    f32, bf16 = jnp.float32, jnp.bfloat16

    def at_pair(xx, zz, cc):
        return zz * 8 + lax.rem(xx + 8, 4) * 2 + cc

    sib = (aux, at_pair(x, zl, 1 - c))
    dev = {
        "x+": (aux, at_pair(x + 1, zl, c)),
        "x-": (aux, at_pair(x - 1, zl, c)),
        "y+": (zh * 4 + lax.rem(y + 1, 4), pair),
        "y-": (zh * 4 + lax.rem(y + 3, 4), pair),
        "zi": (aux, at_pair(x, 1 - zl, c)),
        "zo": ((1 - zh) * 4 + y, at_pair(x, 1 - zl, c)),
        "sib": sib,
    }

    own = pl.ds(pl.multiple_of(pair * nb, nb), nb)
    load_l = pltpu.make_async_copy(l_hbm, lbuf.at[:, own, :], load_sem.at[0])
    load_l.start()
    load_d = pltpu.make_async_copy(d_hbm, dbuf, load_sem.at[1])
    load_d.start()
    is_src = [aux == q for q in range(2)]
    load_p = [pltpu.make_async_copy(m_hbm.at[pl.ds(0, nk), :], pbuf.at[q], load_sem.at[2]) for q in range(2)]
    load_v = pltpu.make_async_copy(l_hbm.at[0, :, pl.ds(0, nk)], vbuf.at[own, :], load_sem.at[3])
    for q in range(2):
        pl.when(is_src[q])(load_p[q].start)
    pl.when(is_src[1])(load_v.start)
    load_m = pltpu.make_async_copy(m_hbm, out, load_sem.at[4])
    load_m.start()

    barrier = pltpu.get_barrier_semaphore()
    for d in dev.values():
        pl.semaphore_signal(barrier, inc=1, device_id=d, device_id_type=MESH)
    for k in range(1, 8):
        @pl.when(is_src[1])
        def _(k=k):
            pl.semaphore_signal(barrier, inc=1, device_id=(lax.rem(aux + k, 8), pair), device_id_type=MESH)

    @pl.when(jnp.logical_not(is_src[1]))
    def _():
        pl.semaphore_signal(barrier, inc=1, device_id=(1, pair), device_id_type=MESH)
        pl.semaphore_wait(barrier, 8)

    @pl.when(is_src[1])
    def _():
        pl.semaphore_wait(barrier, 14)

    def rows_of(r):
        return pl.ds(*CHUNKS[r])

    def slot(r, first, count=nb):
        if r == "V":
            return vbuf.at[pl.ds(first, count), :]
        return lbuf.at[:, pl.ds(first, count), rows_of(r)]

    def index(r):
        return nchunk if r == "V" else r

    def kind(r):
        return "A" if r == "V" else TYPES[r]

    def parity(r):
        return 0 if r == "V" else TYPES[:r].count("B") % 2

    def message(r, xx, zz, to, sem):
        ref = slot(r, pl.multiple_of(at_pair(xx, zz, c) * nb, nb))
        return pltpu.make_async_remote_copy(ref, ref, l_send.at[index(r)], sem, device_id=to, device_id_type=MESH)

    def send(r, xx, zz, to, name):
        message(r, xx, zz, to, l_recv.at[index(r), name]).start()

    def sibling(r, xx, zz):
        message(r, xx, zz, sib, l_sib.at[index(r)]).start()

    def wait(r, xx, zz, name):
        message(r, xx, zz, sib, l_recv.at[index(r), name]).wait_recv()

    def sign(r, z_dyn):
        return z_dyn if kind(r) == "A" else lax.rem(z_dyn + parity(r), 2)

    def ev_oz(r):
        if r == "V":
            pl.when(jnp.logical_not(is_src[1]))(v_copy(1).wait_recv)
            ev_ou(r)
            ev_od(r)
        send(r, x, zl, dev["zi"], Z)

    def ev_ou(r):
        send(r, x, zl, dev["x+"], M)

    def ev_od(r):
        send(r, x, zl, dev["x-"], PL)
        sibling(r, x, zl)

    def across(r, xx, name):
        if kind(r) == "B":
            send(r, xx, zl, dev["zi"], name)

    def ev_f(r):
        s = sign(r, zl)
        step = 1 - 2 * s
        wait(r, x - step, zl, M + s)
        send(r, x - step, zl, (aux, at_pair(x + step, zl, c)), O)
        sibling(r, x - step, zl)
        across(r, x - step, ZM + s)

    def ev_g(r):
        s = sign(r, zl)
        step = 1 - 2 * s
        wait(r, x + step, zl, PL - s)
        sibling(r, x + step, zl)
        across(r, x + step, ZP - s)

    def ev_o(r):
        wait(r, x + 2, zl, O)
        sibling(r, x + 2, zl)
        across(r, x + 2, ZO)

    def ev_z(r):
        wait(r, x, 1 - zl, Z)
        if kind(r) == "A":
            send(r, x, 1 - zl, dev["x+"], ZM)
            send(r, x, 1 - zl, dev["x-"], ZP)
        sibling(r, x, 1 - zl)

    def ev_zf(r):
        s = sign(r, 1 - zl)
        step = 1 - 2 * s
        wait(r, x - step, 1 - zl, ZM + s)
        if kind(r) == "A":
            send(r, x - step, 1 - zl, (aux, at_pair(x + step, zl, c)), ZO)
        sibling(r, x - step, 1 - zl)

    def ev_zg(r):
        s = sign(r, 1 - zl)
        step = 1 - 2 * s
        wait(r, x + step, 1 - zl, ZP - s)
        sibling(r, x + step, 1 - zl)

    def ev_zo(r):
        wait(r, x + 2, 1 - zl, ZO)
        sibling(r, x + 2, 1 - zl)

    def ev_done(r):
        pltpu.make_async_remote_copy(slot(r, 0, 8 * nb), slot(r, 0, 8 * nb), l_send.at[index(r)], l_sib.at[index(r)],
                                     device_id=sib, device_id_type=MESH).wait_recv()

    def ev_sent(r):
        pltpu.make_async_remote_copy(slot(r, 0, 15 * nb), slot(r, 0, 15 * nb), l_send.at[index(r)], l_sib.at[index(r)],
                                     device_id=sib, device_id_type=MESH).wait_send()

    LINKS = ("y+", "y-", "zo", "zi")
    sent = {a: [] for a in range(8)}

    def p_copy(q, i, k, src, dst, to, sem):
        return pltpu.make_async_remote_copy(src, dst, p_send.at[q, i, k], sem, device_id=dev[to], device_id_type=MESH)

    def pivot(a, name, q, i):
        a_zh, a_y = a // 4, a % 4
        cross, trees = ROUTE[q, i]
        full = pbuf.at[q, pl.ds(i * piece, piece), :]
        first = pbuf.at[q, pl.ds(i * piece, half), :]
        second = pbuf.at[q, pl.ds(i * piece + half, half), :]
        relay = rbuf.at[q, pl.ds(i * half, half), :]
        got, rel = p_recv.at[q, i], r_recv.at[q, i]

        def go(k, src, dst, to, sem):
            copy = p_copy(q, i, k, src, dst, to, sem)
            copy.start()
            sent[a].append((q, i, k, src is full))

        if name == "P":
            p_copy(q, i, 0, full, full, "y+", got).wait_recv()
        if name == "X" or (name == "P" and a_zh == 0 and a_y == cross):
            go(2, second, relay, "zo", rel)
            go(3, first, relay, "zi", rel)
        if name[0] == "P":
            for link in trees[a_zh].get(a_y, ()):
                if name in ("P", "P" + link):
                    go(LINKS.index(link), full, full, link, got)
        if name == "R":
            p_copy(q, i, 4, relay, relay, "zi", rel).wait_recv()
            if a_zh == 0:
                go(4, relay, first, "zo", got)
            else:
                go(4, relay, second, "zi", got)

    def v_copy(k):
        ref = vbuf.at[own, :]
        return pltpu.make_async_remote_copy(ref, ref, v_send.at[k], v_recv.at[0], device_id=(lax.rem(aux + k, 8), pair), device_id_type=MESH)

    def ev_v():
        @pl.when(is_src[1])
        def _():
            load_v.wait()
            for k in range(1, 8):
                v_copy(k).start()

    def halves(v):
        h = v.astype(bf16)
        return h, (v - h.astype(f32)).astype(bf16)

    def dot(a, b):
        return jnp.dot(a, b, preferred_element_type=f32)

    def dot_t(a, b):
        return lax.dot_general(a, b, (((0,), (0,)), ((), ())), preferred_element_type=f32)

    width = 256
    cols = [pl.ds(n * width, width) for n in range(out.shape[1] // width)]

    def solve(q):
        dh, dl = halves(dbuf[q])
        for n in cols:
            if q == 0:
                p = pbuf[0, :, n]
                s = dot(dh, p) + dot(dl, p)
            else:
                w = pbuf[1, :, n].astype(f32) - dot_t(vbuf[...], solved[0, :, n])
                wh, wl = halves(w)
                s = dot(dh, wh) + dot(dl, wh) + dot(dh, wl)
            solved[q, :, n] = s.astype(bf16)

    def product(rows, q, last):
        lq = [lbuf[k, :, rows] for k in range(q, last + 1)]
        for n in cols:
            o = out[rows, n].astype(f32) if q == 0 else acc[rows, n]
            for k in range(q, last + 1):
                o = o - dot_t(lq[k - q], solved[k, :, n])
            if last == 1:
                out[rows, n] = o.astype(bf16)
            else:
                acc[rows, n] = o

    load_l.wait()
    for q in range(2):
        pl.when(is_src[q])(load_p[q].wait)
    ev_v()
    act = {"oz": ev_oz, "ou": ev_ou, "od": ev_od, "z": ev_z, "f": ev_f, "g": ev_g, "o": ev_o,
           "zf": ev_zf, "zg": ev_zg, "zo": ev_zo, "done": ev_done}
    chunks = ["V"] + list(range(nchunk))
    skip = False
    for n, step in enumerate(ORDER):
        name, r = step
        if name in act:
            act[name](r)
        elif name == "S":
            if r == 0:
                load_d.wait()
                load_m.wait()
            solve(r)
        elif name == "A":
            skip = ("B", r) == (ORDER + ((),))[n + 1]
            product(rows_of(r), 0, 1 if skip else 0)
        elif name == "B":
            if not skip:
                product(rows_of(r), 1, 1)
            skip = False
        else:
            @pl.when(aux == name)
            def _(a=name, todo=r):
                for what, q, i in todo:
                    pivot(a, what, q, i)

    for r in chunks:
        ev_sent(r)
    for a in sent:
        @pl.when(aux == a)
        def _(a=a):
            for q, i, k, whole in sent[a]:
                ref = pbuf.at[q, pl.ds(i * piece, piece if whole else half), :]
                p_copy(q, i, k, ref, ref, "y+", p_recv.at[q, i]).wait_send()

    @pl.when(is_src[1])
    def _():
        for k in range(1, 8):
            v_copy(k).wait_send()


def finish(part, lbuf, solved, out_hbm, solved_hbm, late, sems):
    f32, bf16 = jnp.float32, jnp.bfloat16
    n_sem = iter(range(2 + len(CHUNKS)))
    copies = [pltpu.make_async_copy(solved, solved_hbm, sems.at[next(n_sem)])]
    ready = sorted(CHUNKS[r] for r in range(len(CHUNKS)) if r not in TAIL)
    runs = []
    for start, size in ready:
        if runs and runs[-1][0] + runs[-1][1] == start:
            runs[-1][1] += size
        else:
            runs.append([start, size])
    for start, size in runs:
        rows = pl.ds(start, size)
        copies.append(pltpu.make_async_copy(part.at[rows, :], out_hbm.at[rows, :], sems.at[next(n_sem)]))
    for copy in copies:
        copy.start()
    base = 0
    width = 256
    for r in TAIL:
        start, size = CHUNKS[r]
        rows = pl.ds(start, size)
        lq = [lbuf[k, :, rows] for k in range(2)]
        for c in range(part.shape[1] // width):
            n = pl.ds(c * width, width)
            o = part[rows, n].astype(f32)
            for k in range(2):
                o = o - lax.dot_general(lq[k], solved[k, :, n], (((0,), (0,)), ((), ())), preferred_element_type=f32)
            late[pl.ds(base, size), n] = o.astype(bf16)
        copy = pltpu.make_async_copy(late.at[pl.ds(base, size), :], out_hbm.at[rows, :], sems.at[next(n_sem)])
        copy.start()
        copies.append(copy)
        base += size
    for copy in copies:
        copy.wait()


def solution(mesh):
    def step(m_panels, lower_cols, diag_inverses):
        rows, cols = m_panels.shape
        panels, nk, _ = diag_inverses.shape
        dma = pltpu.SemaphoreType.DMA
        n = len(TYPES) + 1
        bf16 = jnp.bfloat16
        part, solved, lbuf = pl.pallas_call(
            kernel,
            out_shape=(
                pltpu.VMEM((rows, cols), bf16),
                pltpu.VMEM((panels, nk, cols), bf16),
                pltpu.VMEM((panels, nk, rows), bf16),
            ),
            in_specs=[pl.BlockSpec(memory_space=pltpu.HBM)] * 3,
            out_specs=(pl.BlockSpec(memory_space=pltpu.VMEM),) * 3,
            scratch_shapes=[
                pltpu.VMEM((panels, nk, cols), bf16),
                pltpu.VMEM((panels, nk // 2, cols), bf16),
                pltpu.VMEM((nk, nk), bf16),
                pltpu.VMEM((panels, nk, nk), jnp.float32),
                pltpu.VMEM((rows, cols), jnp.float32),
                dma((5,)), dma((n, 7)), dma((n,)), dma((n,)), dma((1,)), dma((8,)),
                dma((panels, NP)), dma((panels, NP)), dma((panels, NP, 5)),
            ],
            compiler_params=pltpu.CompilerParams(collective_id=0, has_side_effects=True, vmem_limit_bytes=36 * 2**20),
        )(m_panels, lower_cols, diag_inverses)
        late = -(-sum(CHUNKS[r][1] for r in TAIL) // 16) * 16
        return pl.pallas_call(
            finish,
            out_shape=(jax.ShapeDtypeStruct((rows, cols), bf16), jax.ShapeDtypeStruct((panels, nk, cols), bf16)),
            in_specs=[pl.BlockSpec(memory_space=pltpu.VMEM)] * 3,
            out_specs=(pl.BlockSpec(memory_space=pltpu.HBM),) * 2,
            scratch_shapes=[pltpu.VMEM((late, cols), bf16), dma((2 + len(CHUNKS),))],
            compiler_params=pltpu.CompilerParams(vmem_limit_bytes=12 * 2**20),
        )(*(pltpu.with_memory_space_constraint(v, pltpu.VMEM) for v in (part, lbuf, solved)))

    return jax.shard_map(
        step,
        mesh=mesh,
        in_specs=(P("aux", "pair"), P(None, "pair", "aux"), P()),
        out_specs=(P("aux", "pair"), P(None, None, "pair")),
        check_vma=False,
    )
```

profile of v0, /device:TPU:32, one launch (start us, length us, event | category | flops | bytes accessed | tf_op | source)
XLA Modules:
  0.0 65.4 jit_solution(16381558229693727479)
XLA Ops:
  0.6 59.9 %shard_map.50 = (bf16[5000,1024]{1,0:T(8,128)(2,1)S(1)}, bf16[2,512,1024]{2,1,0:T(8,128)(2,1)S(1)}, bf16[2,512,5000]{2,1,0:T(8,128)(2,1)S(1)}) custom-call(bf16[5000,1024]{1,0:T(8,128)(2,1)} %m_hbm.1, bf16[2,32,5000]{2,1,0:T(8,128)(2,1)} %l_hbm.1, f32[2,512,512]{2,1,0:T(8,128)} %d_hbm.1), custom_call_target="tpu_custom_call" | custom-call | tf_op jit(solution)/shard_map/pallas_call | solution.py:599
  60.5 4.7 %shard_map.51 = (bf16[5000,1024]{1,0:T(8,128)(2,1)}, bf16[2,512,1024]{2,1,0:T(8,128)(2,1)}) custom-call(bf16[5000,1024]{1,0:T(8,128)(2,1)S(1)} %get-tuple-element.5.part, bf16[2,512,5000]{2,1,0:T(8,128)(2,1)S(1)} %get-tuple-element.6.lbuf, bf16[2,512,1024]{2,1,0:T(8,128)(2,1)S(1)} %get-tuple-element.7.solved), custom_call_target="tpu_custom_call" | custom-call | tf_op jit(solution)/shard_map/pallas_call | solution.py:620
where the time goes:
time: 65.7 us; the launch traced here: 65.4 us
  Pallas kernels  64.6 us (98%)
  between operations  0.8 us (1%)
    pallas_call x1, Pallas kernels, step(): pl.pallas_call(kernel, out_shape=(pltpu.VMEM((rows, cols), bf16), pltpu.V...  59.9 us
    pallas_call x1, Pallas kernels, step(): pl.pallas_call(finish, out_shape=(jax.ShapeDtypeStruct((rows, cols), bf16...  4.69 us

commit v1 on v0

--- a/solution.py
+++ b/solution.py
@@ -11,234 +11,246 @@
 TYPES = "AABAABAA"
 NP = 8
 ORDER = (
-    (0, (('Py+', 0, 1), ('Py+', 0, 0), ('Py-', 0, 0), ('Py-', 0, 3), ('X', 0, 5), ('X', 0, 6), ('X', 0, 7))),
-    (1, (('Py+', 1, 0), ('Py+', 1, 2), ('Py-', 1, 0), ('Py-', 1, 1), ('X', 1, 4), ('X', 1, 6), ('X', 1, 7))),
+    ('ou', 0),
+    (0, (('X', 0, 6), ('Py+', 0, 0), ('Py+', 0, 1), ('Py-', 0, 0), ('Py-', 0, 3))),
+    (1, (('Py-', 1, 0), ('Py+', 1, 0), ('Py+', 1, 2), ('Py-', 1, 1), ('X', 1, 4), ('X', 1, 6), ('X', 1, 7))),
     ('od', 0),
     ('od', 1),
     ('od', 2),
-    ('od', 3),
     ('od', 4),
     ('od', 5),
     ('od', 6),
     ('od', 7),
-    ('ou', 0),
     ('ou', 1),
+    (0, (('X', 0, 5),)),
+    ('ou', 2),
+    (0, (('X', 0, 7),)),
+    ('oz', 1),
     ('oz', 0),
-    ('ou', 2),
-    ('oz', 1),
+    ('od', 3),
+    ('oz', 2),
     (0, (('Py+', 0, 2), ('Py-', 0, 4), ('R', 0, 5))),
-    (1, (('Py+', 1, 3), ('Py-', 1, 3), ('R', 1, 4))),
+    (1, (('Py-', 1, 3), ('Py+', 1, 3), ('Py+', 1, 5), ('R', 1, 4))),
     (4, (('R', 0, 5),)),
     (5, (('R', 1, 4),)),
-    ('oz', 2),
     ('g', 0),
     ('f', 0),
-    ('oz', 'V'),
-    (0, (('P', 1, 0), ('R', 0, 6), ('Py+', 0, 3))),
-    (1, (('R', 1, 6), ('P', 0, 0), ('Py-', 1, 4))),
+    (0, (('P', 1, 0), ('R', 0, 6), ('Py+', 0, 3), ('Py-', 0, 5))),
+    (1, (('P', 0, 0), ('R', 1, 6), ('Py-', 1, 4))),
     (2, (('P', 1, 0),)),
     (3, (('P', 0, 0),)),
     (4, (('R', 0, 6),)),
     (5, (('R', 1, 6),)),
     ('f', 1),
-    ('g', 1),
-    (0, (('R', 0, 7), ('P', 1, 1), ('Py+', 0, 4), ('Py-', 0, 5))),
-    (1, (('R', 1, 7), ('P', 0, 1), ('Py-', 1, 5))),
+    (0, (('R', 0, 7),)),
+    (1, (('R', 1, 7),)),
+    (4, (('R', 0, 7),)),
+    (5, (('R', 1, 7), ('P', 1, 4))),
+    ('oz', 'V'),
+    ('g', 2),
+    ('f', 2),
+    (0, (('P', 1, 1),)),
+    (1, (('P', 0, 1),)),
     (2, (('P', 1, 2),)),
     (3, (('P', 0, 3),)),
-    (4, (('R', 0, 7),)),
-    (5, (('R', 1, 7),)),
-    ('z', 0),
-    ('g', 2),
-    ('f', 2),
+    ('oz', 3),
+    (0, (('Py+', 0, 4),)),
+    (1, (('Py+', 1, 6), ('Py-', 1, 5))),
+    ('g', 1),
     (4, (('P', 0, 5),)),
-    (5, (('P', 1, 4),)),
     (6, (('R', 1, 0),)),
     (7, (('R', 0, 0),)),
+    ('z', 0),
+    (0, (('Py-', 0, 6),)),
+    (2, (('R', 1, 0),)),
+    ('ou', 3),
     ('z', 1),
-    (0, (('P', 1, 3), ('Py+', 0, 5))),
-    (1, (('P', 0, 2), ('Py+', 1, 5), ('Py-', 1, 7))),
-    (2, (('R', 1, 0), ('P', 0, 0), ('P', 1, 3))),
-    (3, (('R', 0, 0), ('P', 0, 4))),
-    ('ou', 3),
-    ('oz', 3),
-    (1, (('P', 0, 3),)),
-    (2, (('R', 1, 2),)),
-    (3, (('R', 0, 3), ('P', 1, 2))),
-    (4, (('P', 0, 6), ('R', 1, 1))),
-    (5, (('P', 1, 6), ('R', 0, 1))),
+    (0, (('Py+', 0, 5), ('P', 1, 3), ('Py-', 0, 7))),
+    (1, (('P', 0, 2), ('Py+', 1, 7), ('Py-', 1, 7))),
+    (2, (('P', 0, 0), ('P', 1, 3))),
+    (3, (('P', 0, 4),)),
+    (4, (('P', 0, 6),)),
+    (5, (('P', 1, 6),)),
+    ('ou', 4),
+    ('z', 2),
+    (3, (('R', 0, 0),)),
+    (4, (('R', 1, 1), ('P', 0, 7))),
+    (5, (('R', 0, 1),)),
     (6, (('R', 1, 2),)),
     (7, (('R', 0, 3),)),
-    ('z', 2),
     ('z', 'V'),
-    (0, (('P', 1, 4), ('Py+', 0, 6), ('R', 1, 1))),
-    (1, (('Py+', 1, 6), ('R', 0, 1))),
-    (2, (('P', 0, 3), ('P', 0, 1))),
-    (3, (('P', 1, 1),)),
-    (4, (('P', 0, 7),)),
     (5, (('P', 1, 7), ('R', 0, 2))),
+    ('zg', 2),
+    (2, (('P', 0, 3),)),
+    (3, (('P', 1, 2),)),
+    ('oz', 4),
+    (0, (('P', 1, 4), ('Py+', 0, 6))),
+    (1, (('P', 0, 3),)),
+    (2, (('P', 1, 5),)),
+    (3, (('P', 0, 5),)),
     (6, (('P', 1, 4),)),
-    ('ou', 4),
-    (3, (('P', 1, 3),)),
+    ('oz', 5),
+    (2, (('R', 1, 2),)),
+    (3, (('P', 1, 0), ('R', 0, 3))),
     (4, (('P', 1, 4),)),
     (5, (('P', 0, 5),)),
     (6, (('R', 1, 3),)),
     (7, (('P', 0, 5), ('R', 0, 4))),
     ('g', 3),
-    ('oz', 4),
-    (0, (('P', 1, 5), ('Py+', 0, 7), ('Py-', 0, 6))),
-    (1, (('Py+', 1, 7),)),
-    (2, (('P', 0, 4), ('P', 0, 2))),
-    (3, (('P', 1, 0), ('P', 0, 5))),
+    ('zf', 2),
+    (0, (('P', 1, 5), ('Py+', 0, 7))),
+    (2, (('P', 0, 4), ('P', 0, 1))),
+    (3, (('P', 1, 3), ('P', 1, 1))),
+    (7, (('P', 0, 0),)),
+    ('g', 'V'),
+    (0, (('R', 1, 1),)),
+    (1, (('R', 0, 1), ('P', 0, 4))),
+    (3, (('R', 0, 4),)),
     (5, (('P', 0, 6),)),
-    ('g', 'V'),
-    (1, (('P', 0, 4),)),
-    ('zg', 2),
-    (6, (('P', 1, 0), ('P', 1, 6))),
-    (7, (('P', 0, 0),)),
+    (6, (('P', 1, 6), ('R', 1, 5), ('P', 1, 0))),
+    (7, (('P', 0, 6),)),
     ('o', 0),
+    (4, (('P', 1, 7),)),
+    ('f', 3),
+    (0, (('P', 1, 2),)),
     (2, (('R', 1, 3),)),
-    (3, (('R', 0, 4),)),
-    (7, (('P', 0, 6),)),
     ('zf', 0),
     ('f', 'V'),
+    (2, (('P', 0, 5),)),
+    ('o', 1),
+    (0, (('P', 1, 7),)),
+    (1, (('P', 0, 5),)),
+    (2, (('P', 1, 6),)),
+    (3, (('P', 0, 6),)),
+    (6, (('P', 1, 2),)),
+    ('z', 3),
     ('ou', 5),
-    (0, (('P', 1, 2),)),
-    ('oz', 5),
-    (0, (('P', 1, 7), ('Py-', 0, 7))),
-    (1, (('P', 0, 5),)),
-    (2, (('P', 1, 1), ('P', 1, 5))),
-    (3, (('P', 0, 1), ('P', 1, 4))),
-    (4, (('P', 1, 7),)),
+    (7, (('P', 0, 3), ('P', 1, 4))),
+    ('zf', 'V'),
+    (5, (('P', 0, 7),)),
+    (6, (('P', 0, 5),)),
+    (7, (('P', 0, 7),)),
+    ('oz', 6),
     ('zf', 1),
-    ('zf', 2),
-    (7, (('P', 0, 3),)),
+    (1, (('R', 0, 2),)),
     ('g', 4),
-    ('f', 3),
-    (1, (('R', 0, 2),)),
-    (5, (('P', 0, 7),)),
-    (6, (('P', 1, 2), ('P', 0, 5))),
-    (7, (('P', 1, 4), ('P', 0, 7))),
-    ('zf', 'V'),
-    (2, (('P', 0, 5),)),
-    (3, (('P', 0, 2),)),
     (4, (('P', 1, 1),)),
-    (5, (('P', 0, 1),)),
-    ('zg', 0),
+    (5, (('P', 0, 1), ('P', 1, 0))),
+    ('f', 4),
     (1, (('P', 0, 6),)),
-    (2, (('P', 1, 6),)),
-    (3, (('P', 1, 5),)),
+    (2, (('P', 1, 1),)),
+    (3, (('P', 0, 7),)),
     (4, (('P', 0, 0),)),
-    (5, (('P', 1, 0),)),
     (6, (('P', 0, 0),)),
     (7, (('P', 0, 4),)),
-    ('z', 3),
-    ('f', 4),
+    ('oz', 7),
     ('zo', 0),
+    (6, (('P', 0, 6), ('P', 1, 3))),
+    ('o', 2),
+    (2, (('P', 0, 2),)),
+    (3, (('P', 0, 1),)),
+    (7, (('P', 1, 7),)),
+    ('ou', 6),
+    (2, (('R', 1, 5),)),
+    ('zg', 0),
+    ('z', 5),
+    (5, (('P', 0, 2),)),
     (7, (('P', 1, 0),)),
-    ('o', 1),
-    (6, (('P', 1, 3), ('R', 1, 5))),
-    ('ou', 6),
-    (6, (('P', 0, 6),)),
+    ('z', 4),
+    (2, (('P', 0, 6),)),
+    (3, (('P', 1, 6), ('P', 1, 4))),
+    ('zf', 3),
+    (1, (('P', 0, 7),)),
+    (4, (('P', 0, 3),)),
+    (6, (('P', 0, 3),)),
     ('done', 0),
-    (7, (('P', 1, 7),)),
-    ('z', 4),
-    ('o', 2),
-    (1, (('P', 0, 7),)),
-    (2, (('P', 1, 4),)),
-    (3, (('P', 0, 6),)),
-    ('f', 5),
-    (2, (('R', 1, 5),)),
-    (4, (('P', 0, 3),)),
-    (5, (('P', 0, 2), ('P', 1, 2))),
-    (6, (('P', 0, 3),)),
-    ('g', 5),
+    (6, (('P', 1, 5),)),
     (7, (('P', 1, 6),)),
     ('zg', 1),
+    ('f', 5),
+    (2, (('P', 1, 7),)),
     (4, (('P', 0, 1),)),
+    (5, (('P', 1, 2), ('P', 1, 1))),
+    ('z', 6),
+    (6, (('P', 0, 7),)),
+    ('o', 'V'),
+    ('g', 5),
+    (3, (('P', 0, 2), ('P', 1, 5))),
     ('zo', 1),
-    (5, (('P', 1, 1),)),
-    (6, (('P', 0, 7),)),
+    ('zg', 'V'),
+    (6, (('P', 0, 4),)),
+    (7, (('P', 1, 2),)),
+    ('zo', 'V'),
+    ('zo', 2),
+    (6, (('P', 0, 1),)),
+    ('ou', 7),
+    (5, (('P', 1, 3),)),
+    (6, (('P', 0, 2),)),
     (7, (('P', 1, 1),)),
     ('done', 1),
-    ('o', 'V'),
-    ('zg', 'V'),
-    ('oz', 6),
-    (2, (('P', 1, 7),)),
-    ('zo', 'V'),
-    (3, (('P', 1, 6), ('P', 0, 7))),
-    ('ou', 7),
+    ('z', 7),
+    ('done', 'V'),
+    ('done', 2),
     (4, (('P', 0, 4),)),
-    ('oz', 7),
-    (5, (('P', 1, 3),)),
-    (6, (('P', 0, 4),)),
-    ('z', 5),
-    (7, (('P', 1, 2),)),
-    ('zf', 3),
     (5, (('P', 0, 0),)),
-    (6, (('P', 0, 1),)),
     ('o', 3),
-    ('zo', 2),
-    (2, (('P', 0, 7), ('P', 0, 6))),
+    ('zg', 3),
+    (0, (('P', 1, 6),)),
+    (2, (('P', 0, 7),)),
     (3, (('P', 1, 7),)),
-    (4, (('P', 0, 2),)),
-    (6, (('P', 1, 5),)),
+    (4, (('P', 0, 2), ('P', 1, 0))),
+    (7, (('P', 1, 3),)),
+    ('o', 4),
+    (5, (('P', 1, 5),)),
+    ('zf', 5),
+    (5, (('P', 0, 3),)),
+    (6, (('P', 1, 7),)),
+    (7, (('P', 0, 1),)),
+    ('zg', 5),
+    ('f', 6),
+    ('zo', 3),
     ('zf', 4),
-    (0, (('P', 1, 6),)),
-    (4, (('P', 1, 0),)),
-    ('zg', 3),
-    ('done', 2),
-    (5, (('P', 0, 3),)),
-    (6, (('P', 1, 7), ('P', 0, 2))),
-    (7, (('P', 1, 3), ('P', 0, 1))),
+    (4, (('P', 1, 6),)),
+    (7, (('P', 1, 5),)),
+    ('zg', 4),
+    (4, (('P', 1, 3),)),
+    (5, (('P', 0, 4),)),
+    (6, (('P', 1, 1),)),
+    ('done', 3),
+    ('o', 5),
     ('g', 6),
-    ('o', 4),
-    ('done', 'V'),
-    ('f', 6),
-    ('o', 5),
-    (4, (('P', 1, 6), ('P', 1, 3))),
-    (6, (('P', 1, 1),)),
     ('f', 7),
-    ('zg', 4),
-    ('zg', 5),
-    ('g', 7),
-    ('zf', 5),
-    ('z', 6),
-    (5, (('P', 0, 4),)),
+    ('zg', 6),
     (7, (('P', 0, 2),)),
     ('S', 0),
-    (7, (('P', 1, 5),)),
-    ('z', 7),
+    (2, (('P', 1, 4),)),
     (4, (('P', 1, 2),)),
-    ('zo', 3),
-    (5, (('P', 1, 5),)),
+    ('zf', 6),
     ('A', 0),
+    ('g', 7),
+    ('A', 1),
+    ('A', 2),
+    (4, (('P', 1, 5),)),
+    ('zo', 5),
+    ('o', 7),
+    ('zf', 7),
+    ('zg', 7),
+    ('S', 1),
+    ('zo', 4),
     ('o', 6),
-    ('A', 1),
-    ('zo', 4),
-    ('done', 3),
-    ('o', 7),
-    ('zf', 6),
-    ('A', 2),
-    ('zo', 5),
-    ('zg', 6),
     ('A', 3),
-    ('zg', 7),
+    ('done', 5),
+    ('A', 5),
+    ('zo', 6),
+    ('B', 0),
+    ('B', 1),
+    ('zo', 7),
+    ('B', 2),
+    ('done', 6),
+    ('B', 3),
+    ('B', 5),
+    ('done', 7),
     ('done', 4),
-    ('zf', 7),
-    ('A', 4),
-    ('zo', 6),
-    (4, (('P', 1, 5),)),
-    ('S', 1),
-    ('zo', 7),
-    ('done', 6),
-    ('done', 5),
-    ('B', 0),
-    ('done', 7),
-    ('B', 1),
-    ('B', 2),
-    ('B', 3),
-    ('B', 4),
 )
 ROUTE = {
     (0, 0): (3, {0: {0: ['y+', 'y-'], 3: ['y-']}, 1: {3: ['y+', 'y-'], 0: ['y+']}}),
@@ -258,13 +270,13 @@
     (1, 6): (1, {0: {1: ['y+'], 2: ['y+'], 3: ['y+']}, 1: {1: ['y+'], 2: ['y+'], 3: ['y+']}}),
     (1, 7): (1, {0: {1: ['y+', 'y-'], 2: ['y+']}, 1: {1: ['y-'], 0: ['y-'], 3: ['y-']}}),
 }
-CHUNKS = ((0, 640), (640, 640), (1280, 896), (2176, 640), (2816, 640), (3456, 896), (4352, 384), (4736, 264))
-TAIL = (5, 6, 7)
+CHUNKS = ((0, 640), (640, 640), (1280, 640), (1920, 640), (2560, 640), (3200, 640), (3840, 640), (4480, 520))
+TAIL = (4, 6, 7)
 Z, M, PL, O, ZM, ZP, ZO = range(7)
 
 
 def kernel(m_hbm, l_hbm, d_hbm, out, solved, lbuf, pbuf, rbuf, vbuf, dbuf, acc,
-           load_sem, l_recv, l_sib, l_send, v_recv, v_send, p_recv, r_recv, p_send):
+           load_sem, l_recv, l_sib, l_send, v_recv, v_send, p_recv, r_recv, p_send, ready_sem):
     aux, pair = lax.axis_index("aux"), lax.axis_index("pair")
     zh, y = aux // 4, aux % 4
     zl, x, c = pair // 8, (pair // 2) % 4, pair % 2
@@ -314,12 +326,12 @@
 
     @pl.when(jnp.logical_not(is_src[1]))
     def _():
-        pl.semaphore_signal(barrier, inc=1, device_id=(1, pair), device_id_type=MESH)
         pl.semaphore_wait(barrier, 8)
+        pl.semaphore_signal(ready_sem, inc=1, device_id=(1, pair), device_id_type=MESH)
 
     @pl.when(is_src[1])
     def _():
-        pl.semaphore_wait(barrier, 14)
+        pl.semaphore_wait(barrier, 7)
 
     def rows_of(r):
         return pl.ds(*CHUNKS[r])
@@ -469,6 +481,7 @@
         @pl.when(is_src[1])
         def _():
             load_v.wait()
+            pl.semaphore_wait(ready_sem, 7)
             for k in range(1, 8):
                 v_copy(k).start()
 
@@ -511,12 +524,13 @@
     load_l.wait()
     for q in range(2):
         pl.when(is_src[q])(load_p[q].wait)
-    ev_v()
     act = {"oz": ev_oz, "ou": ev_ou, "od": ev_od, "z": ev_z, "f": ev_f, "g": ev_g, "o": ev_o,
            "zf": ev_zf, "zg": ev_zg, "zo": ev_zo, "done": ev_done}
     chunks = ["V"] + list(range(nchunk))
     skip = False
     for n, step in enumerate(ORDER):
+        if n == 15:
+            ev_v()
         name, r = step
         if name in act:
             act[name](r)
@@ -612,7 +626,7 @@
                 pltpu.VMEM((panels, nk, nk), jnp.float32),
                 pltpu.VMEM((rows, cols), jnp.float32),
                 dma((5,)), dma((n, 7)), dma((n,)), dma((n,)), dma((1,)), dma((8,)),
-                dma((panels, NP)), dma((panels, NP)), dma((panels, NP, 5)),
+                dma((panels, NP)), dma((panels, NP)), dma((panels, NP, 5)), pltpu.SemaphoreType.REGULAR,
             ],
             compiler_params=pltpu.CompilerParams(collective_id=0, has_side_effects=True, vmem_limit_bytes=36 * 2**20),
         )(m_panels, lower_cols, diag_inverses)

time: 65.7 us -> 64.8 us (0.986)
  Pallas kernels: 64.6 us -> 63.9 us
    pallas_call x1, Pallas kernels: 59.9 us -> 58.8 us  [step(): pl.pallas_call(kernel, out_shape=(pltpu.VMEM((rows, cols), bf16), pltpu.V...]
where the time goes in v1:
time: 64.8 us; the launch traced here: 64.7 us
  Pallas kernels  63.9 us (99%)
  between operations  0.8 us (1%)
    pallas_call x1, Pallas kernels, step(): pl.pallas_call(kernel, out_shape=(pltpu.VMEM((rows, cols), bf16), pltpu.V...  58.8 us
    pallas_call x1, Pallas kernels, step(): pl.pallas_call(finish, out_shape=(jax.ShapeDtypeStruct((rows, cols), bf16...  5.13 us

profile of v1, /device:TPU:32, one launch (start us, length us, event | category | flops | bytes accessed | tf_op | source)
XLA Modules:
  0.0 64.7 jit_solution(10636151878131831011)
XLA Ops:
  0.6 58.8 %shard_map.50 = (bf16[5000,1024]{1,0:T(8,128)(2,1)S(1)}, bf16[2,512,1024]{2,1,0:T(8,128)(2,1)S(1)}, bf16[2,512,5000]{2,1,0:T(8,128)(2,1)S(1)}) custom-call(bf16[5000,1024]{1,0:T(8,128)(2,1)} %m_hbm.1, bf16[2,32,5000]{2,1,0:T(8,128)(2,1)} %l_hbm.1, f32[2,512,512]{2,1,0:T(8,128)} %d_hbm.1), custom_call_target="tpu_custom_call" | custom-call | tf_op jit(solution)/shard_map/pallas_call | solution.py:613
  59.4 5.1 %shard_map.51 = (bf16[5000,1024]{1,0:T(8,128)(2,1)}, bf16[2,512,1024]{2,1,0:T(8,128)(2,1)}) custom-call(bf16[5000,1024]{1,0:T(8,128)(2,1)S(1)} %get-tuple-element.5.part, bf16[2,512,5000]{2,1,0:T(8,128)(2,1)S(1)} %get-tuple-element.6.lbuf, bf16[2,512,1024]{2,1,0:T(8,128)(2,1)S(1)} %get-tuple-element.7.solved), custom_call_target="tpu_custom_call" | custom-call | tf_op jit(solution)/shard_map/pallas_call | solution.py:634

commit v2 on v1

--- a/solution.py
+++ b/solution.py
@@ -569,7 +569,7 @@
 
 def finish(part, lbuf, solved, out_hbm, solved_hbm, late, sems):
     f32, bf16 = jnp.float32, jnp.bfloat16
-    n_sem = iter(range(2 + len(CHUNKS)))
+    n_sem = iter(range(2 + 2 * len(CHUNKS)))
     copies = [pltpu.make_async_copy(solved, solved_hbm, sems.at[next(n_sem)])]
     ready = sorted(CHUNKS[r] for r in range(len(CHUNKS)) if r not in TAIL)
     runs = []
@@ -595,9 +595,11 @@
             for k in range(2):
                 o = o - lax.dot_general(lq[k], solved[k, :, n], (((0,), (0,)), ((), ())), preferred_element_type=f32)
             late[pl.ds(base, size), n] = o.astype(bf16)
-        copy = pltpu.make_async_copy(late.at[pl.ds(base, size), :], out_hbm.at[rows, :], sems.at[next(n_sem)])
-        copy.start()
-        copies.append(copy)
+            if c % 2:
+                pair_cols = pl.ds((c - 1) * width, 2 * width)
+                copy = pltpu.make_async_copy(late.at[pl.ds(base, size), pair_cols], out_hbm.at[rows, pair_cols], sems.at[next(n_sem)])
+                copy.start()
+                copies.append(copy)
         base += size
     for copy in copies:
         copy.wait()
@@ -636,7 +638,7 @@
             out_shape=(jax.ShapeDtypeStruct((rows, cols), bf16), jax.ShapeDtypeStruct((panels, nk, cols), bf16)),
             in_specs=[pl.BlockSpec(memory_space=pltpu.VMEM)] * 3,
             out_specs=(pl.BlockSpec(memory_space=pltpu.HBM),) * 2,
-            scratch_shapes=[pltpu.VMEM((late, cols), bf16), dma((2 + len(CHUNKS),))],
+            scratch_shapes=[pltpu.VMEM((late, cols), bf16), dma((2 + 2 * len(CHUNKS),))],
             compiler_params=pltpu.CompilerParams(vmem_limit_bytes=12 * 2**20),
         )(*(pltpu.with_memory_space_constraint(v, pltpu.VMEM) for v in (part, lbuf, solved)))
 

time: 64.8 us -> 64.7 us (level)
  no operation moved by 1% of the time
where the time goes in v2:
time: 64.7 us; the launch traced here: 64.6 us
  Pallas kernels  63.8 us (99%)
  between operations  0.8 us (1%)
    pallas_call x1, Pallas kernels, step(): pl.pallas_call(kernel, out_shape=(pltpu.VMEM((rows, cols), bf16), pltpu.V...  58.8 us
    pallas_call x1, Pallas kernels, step(): pl.pallas_call(finish, out_shape=(jax.ShapeDtypeStruct((rows, cols), bf16...  5.02 us

profile of v2, /device:TPU:32, one launch (start us, length us, event | category | flops | bytes accessed | tf_op | source)
XLA Modules:
  0.0 64.6 jit_solution(7139701966596297919)
XLA Ops:
  0.6 58.8 %shard_map.50 = (bf16[5000,1024]{1,0:T(8,128)(2,1)S(1)}, bf16[2,512,1024]{2,1,0:T(8,128)(2,1)S(1)}, bf16[2,512,5000]{2,1,0:T(8,128)(2,1)S(1)}) custom-call(bf16[5000,1024]{1,0:T(8,128)(2,1)} %m_hbm.1, bf16[2,32,5000]{2,1,0:T(8,128)(2,1)} %l_hbm.1, f32[2,512,512]{2,1,0:T(8,128)} %d_hbm.1), custom_call_target="tpu_custom_call" | custom-call | tf_op jit(solution)/shard_map/pallas_call | solution.py:615
  59.4 5.0 %shard_map.51 = (bf16[5000,1024]{1,0:T(8,128)(2,1)}, bf16[2,512,1024]{2,1,0:T(8,128)(2,1)}) custom-call(bf16[5000,1024]{1,0:T(8,128)(2,1)S(1)} %get-tuple-element.5.part, bf16[2,512,5000]{2,1,0:T(8,128)(2,1)S(1)} %get-tuple-element.6.lbuf, bf16[2,512,1024]{2,1,0:T(8,128)(2,1)S(1)} %get-tuple-element.7.solved), custom_call_target="tpu_custom_call" | custom-call | tf_op jit(solution)/shard_map/pallas_call | solution.py:636
